TPU v7x, 8 devices: a whole 2x2x1 slice. The times are simulated.
8 devices in a mesh: dp: 1 (over z), sp: 8 (over y, x, core).
Axes of the slice: x: 2, y: 2, z: 1, core: 2. Of those that a mesh axis runs over, the one named last changes fastest.
Arguments:
- x_in: bfloat16 [4096, 4096], P(('dp', 'sp'))
- w_in: bfloat16 [4096, 16768], replicated
- a_neg: float32 [128], replicated
- dt_bias: float32 [128], replicated
- d_skip: float32 [128], replicated
- w_out: bfloat16 [8192, 4096], replicated
Outputs:
- output: bfloat16 [4096, 4096], P(('dp', 'sp'))
All inputs are finite; a program needn't handle non-finite values.
Results may differ from a plain program's by a relative error of at most 0.00344.
Values are sent between devices in bfloat16 or wider.
A program may use at most 1 GiB of HBM per device.

v0:
```python
import jax
import jax.numpy as jnp
from jax import lax
from jax.experimental import pallas as pl
from jax.experimental.pallas import tpu as pltpu
from jax.sharding import PartitionSpec as P

SEG = 128
HEAD_DIM = 64
STATE = 128
TILE = 512
HALF = TILE // 2
TILE_HEADS = TILE // HEAD_DIM
LANES = 128
LAG_X = 8
LAG_Y = 14
LOG2E = 1.4426950408889634
MESH = pl.DeviceIdType.MESH
BF16 = jnp.bfloat16
F32 = jnp.float32


def dot32(a, b):
    return jnp.dot(a, b, preferred_element_type=F32)


def spread(v, pairs):
    rows = v.shape[0]
    low = lax.broadcasted_iota(jnp.int32, (rows, LANES), 1) < HEAD_DIM
    parts = []
    for p in range(pairs):
        left = jnp.broadcast_to(v[:, 2 * p:2 * p + 1], (rows, LANES))
        right = jnp.broadcast_to(v[:, 2 * p + 1:2 * p + 2], (rows, LANES))
        parts.append(jnp.where(low, left, right))
    return jnp.concatenate(parts, axis=1)


def lane_shift(v, first):
    return pltpu.roll(v, lax.rem(LANES - first, LANES), 1)


def project_kernel(x_ref, w_ref, wbc_ref, wdt_ref, an_ref, db_ref,
                   u_ref, xw_ref, bc_ref, bt_ref, gl_ref, qt_ref, dec_ref, hin_ref,
                   wst, lsend, lall, s_own, rc, sx, rx, sy, ry, rf,
                   lsem, lrem, csem, crem, xsem, xrem, ysem, yrem, fsem, frem):
    step = pl.program_id(0)
    me = lax.axis_index("sp")
    tokens = x_ref.shape[0]
    segs = tokens // SEG
    tiles = s_own.shape[0]
    core = lax.rem(me, 2)
    xpos = lax.rem(me // 2, 2)
    ypos = me // 4
    peer_core = me + 1 - 2 * core
    peer_x = me + 2 - 4 * xpos
    peer_y = me + 4 - 8 * ypos
    barrier = pltpu.get_barrier_semaphore()

    def other(k):
        return lax.rem(me + k, 8)

    def log_copy(k):
        return pltpu.make_async_remote_copy(
            src_ref=lsend, dst_ref=lall.at[me], send_sem=lsem.at[k - 1], recv_sem=lrem.at[me],
            device_id={"sp": other(k)}, device_id_type=MESH)

    def remote(src, dst, send, recv, target):
        return pltpu.make_async_remote_copy(
            src_ref=src, dst_ref=dst, send_sem=send, recv_sem=recv,
            device_id={"sp": target}, device_id_type=MESH)

    def core_copy(c):
        return remote(s_own.at[c, 1 - core], rc.at[c], csem.at[c], crem.at[c], peer_core)

    def x_copy(c):
        return remote(sx.at[c], rx.at[c], xsem.at[c], xrem.at[c], peer_x)

    def y_copy(c):
        return remote(sy.at[c], ry.at[c], ysem.at[c], yrem.at[c], peer_y)

    def final_copy(c):
        return remote(sy.at[c], rf.at[c], fsem.at[c], frem.at[c], peer_core)

    def at_lag(lag):
        return jnp.logical_and(step >= lag, step < tiles + lag)

    def decay_row(logs, c):
        first = c * TILE_HEADS + core * (TILE_HEADS // 2)
        return spread(lane_shift(jnp.exp(logs), first), 2)[:1]

    @pl.when(step == 0)
    def _():
        for k in range(1, 8):
            pl.semaphore_signal(barrier, inc=1, device_id={"sp": other(k)}, device_id_type=MESH)
        x = x_ref[...]
        bc = dot32(x, wbc_ref[...]).astype(BF16)
        bc_ref[...] = bc
        raw = dot32(x, wdt_ref[...]).astype(BF16).astype(F32) + db_ref[...]
        dt = jnp.maximum(raw, 0.0) + jnp.log1p(jnp.exp(-jnp.abs(raw)))
        logs = dt * an_ref[...]
        tri = (lax.broadcasted_iota(jnp.int32, (SEG, SEG), 0)
               >= lax.broadcasted_iota(jnp.int32, (SEG, SEG), 1)).astype(F32)
        total = jnp.zeros((1, LANES), F32)
        row = lax.broadcasted_iota(jnp.int32, (8, LANES), 0)
        dec = jnp.zeros((8, LANES), F32)
        for c in range(segs):
            rows = slice(c * SEG, (c + 1) * SEG)
            cum = jnp.dot(tri, logs[rows], precision=lax.Precision.HIGHEST, preferred_element_type=F32)
            last = cum[SEG - 1:SEG]
            wst[rows, :] = jnp.exp(last - cum) * dt[rows]
            gl_ref[rows, :] = cum * LOG2E
            qt_ref[rows, :] = jnp.transpose(cum * LOG2E - jnp.log2(dt[rows]))
            bt_ref[rows, :] = jnp.transpose(bc[rows, :STATE].astype(F32)).astype(BF16)
            dec = jnp.where(row == c, jnp.exp(last), dec)
            total = total + last
        dec_ref[...] = dec
        lsend[...] = jnp.broadcast_to(total, (8, LANES))

    @pl.when(step == 1)
    def _():
        pl.semaphore_wait(barrier, 7)
        for k in range(1, 8):
            log_copy(k).start()
        lall[me] = lsend[...]

    @pl.when(at_lag(1))
    def _():
        core_copy(step - 1).start()

    @pl.when(step == 2)
    def _():
        for k in range(1, 8):
            log_copy(k).wait_send()
            source = other(k)
            pltpu.make_async_remote_copy(
                src_ref=lsend, dst_ref=lall.at[source], send_sem=lsem.at[k - 1], recv_sem=lrem.at[source],
                device_id={"sp": source}, device_id_type=MESH).wait_recv()

    @pl.when(at_lag(2))
    def _():
        c = step - 2
        core_copy(c).wait()
        mine, got = s_own[c, core], rc[c]
        early = jnp.where(core == 0, mine, got)
        late = jnp.where(core == 0, got, mine)
        sx[c] = decay_row(lall[me - core + 1], c) * early + late

    @pl.when(at_lag(3))
    def _():
        x_copy(step - 3).start()

    @pl.when(at_lag(LAG_X))
    def _():
        c = step - LAG_X
        x_copy(c).wait()
        mine, got = sx[c], rx[c]
        early = jnp.where(xpos == 0, mine, got)
        late = jnp.where(xpos == 0, got, mine)
        chip = ypos * 4 + 2
        sy[c] = decay_row(lall[chip] + lall[chip + 1], c) * early + late

    @pl.when(at_lag(LAG_X + 1))
    def _():
        y_copy(step - LAG_X - 1).start()

    @pl.when(at_lag(LAG_Y))
    def _():
        c = step - LAG_Y
        y_copy(c).wait()
        chip = ypos * 4
        logs = jnp.where(xpos == 1, lall[chip] + lall[chip + 1], 0.0)
        before = jnp.where(xpos == 1, rx[c], 0.0) + jnp.where(ypos == 1, decay_row(logs, c) * ry[c], 0.0)
        first = jnp.where(core == 0, s_own[c, core], rc[c])
        after = decay_row(lall[me - core], c) * before + first
        sx[c] = jnp.where(core == 0, before, after)
        sy[c] = jnp.where(core == 0, after, before)

    @pl.when(at_lag(LAG_Y + 1))
    def _():
        final_copy(step - LAG_Y - 1).start()

    @pl.when(at_lag(LAG_Y + 2))
    def _():
        c = step - LAG_Y - 2
        final_copy(c).wait()
        mine, got = sx[c], rf[c]
        hin_ref[:, :HALF] = jnp.where(core == 0, mine, got)
        hin_ref[:, HALF:] = jnp.where(core == 0, got, mine)

    u = dot32(x_ref[...], w_ref[...]).astype(BF16)
    u_ref[...] = u

    @pl.when(step < tiles)
    def _():
        weights = lane_shift(wst[...], step * TILE_HEADS)
        dec = spread(lane_shift(dec_ref[...], step * TILE_HEADS), TILE_HEADS // 2)
        state = jnp.zeros((STATE, TILE), F32)
        for c in range(segs):
            rows = slice(c * SEG, (c + 1) * SEG)
            xw = (u_ref[rows, :].astype(F32) * spread(weights[rows], TILE_HEADS // 2)).astype(BF16)
            xw_ref[rows, :] = xw
            state = dec[c:c + 1] * state + dot32(bt_ref[rows, :], xw)
        s_own[step, 0] = state[:, :HALF]
        s_own[step, 1] = state[:, HALF:]


def mix_kernel(z_ref, xs_ref, xw_ref, h_ref, bc_ref, bt_ref, gl_ref, qt_ref, dec_ref, ds_ref, x_ref, wo_ref,
               out_ref, acc, gated, scores):
    group = pl.program_id(0)
    groups = pl.num_programs(0)
    tokens = x_ref.shape[0]
    segs = tokens // SEG

    @pl.when(group == 0)
    def _():
        acc[...] = x_ref[...].astype(F32)
        for c in range(segs):
            rows = slice(c * SEG, (c + 1) * SEG)
            scores[rows, :] = lax.dot_general(bc_ref[rows, STATE:], bc_ref[rows, :STATE],
                                              (((1,), (1,)), ((), ())), preferred_element_type=F32)

    first = group * TILE_HEADS
    gl = lane_shift(gl_ref[...], first)
    dec = spread(lane_shift(dec_ref[...], first), TILE_HEADS // 2)
    skip = spread(lane_shift(jnp.broadcast_to(ds_ref[...], (8, LANES)), first), TILE_HEADS // 2)[:1]
    causal = (lax.broadcasted_iota(jnp.int32, (SEG, SEG), 0)
              >= lax.broadcasted_iota(jnp.int32, (SEG, SEG), 1))
    low = lax.broadcasted_iota(jnp.int32, (SEG, LANES), 1) < HEAD_DIM
    zero = jnp.zeros((SEG, LANES), BF16)
    state = h_ref[...]
    for c in range(segs):
        rows = slice(c * SEG, (c + 1) * SEG)
        y_state = dot32(bc_ref[rows, STATE:], state.astype(BF16))
        if c < segs - 1:
            state = dec[c:c + 1] * state + dot32(bt_ref[rows, :], xw_ref[rows, :])
        q_rows = qt_ref[pl.ds(pl.multiple_of(c * SEG + first, TILE_HEADS), TILE_HEADS), :]
        sc = scores[rows, :]
        for p in range(TILE_HEADS // 2):
            cols = slice(p * LANES, (p + 1) * LANES)
            col_a = jnp.broadcast_to(gl[rows, 2 * p:2 * p + 1], (SEG, LANES))
            col_b = jnp.broadcast_to(gl[rows, 2 * p + 1:2 * p + 2], (SEG, LANES))
            g_a = jnp.where(causal, sc * jnp.exp2(col_a - q_rows[2 * p:2 * p + 1]), 0.0).astype(BF16)
            g_b = jnp.where(causal, sc * jnp.exp2(col_b - q_rows[2 * p + 1:2 * p + 2]), 0.0).astype(BF16)
            xp = xs_ref[rows, cols]
            rhs = jnp.concatenate([jnp.where(low, xp, zero), jnp.where(low, zero, xp)], axis=0)
            y = dot32(jnp.concatenate([g_a, g_b], axis=1), rhs)
            y = y + y_state[:, cols] * jnp.exp2(jnp.where(low, col_a, col_b)) + skip[:, cols] * xp.astype(F32)
            z = z_ref[rows, cols].astype(F32)
            gated[rows, cols] = (y * (z / (1.0 + jnp.exp(-z)))).astype(BF16)

    acc[...] += dot32(gated[...], wo_ref[...])

    @pl.when(group == groups - 1)
    def _():
        out_ref[...] = acc[...].astype(BF16)


def solution(mesh):
    row_spec = P(("dp", "sp"), None)

    def local_mixer(x_loc, w_in, a_neg, dt_bias, d_skip, w_out):
        tokens, d_model = x_loc.shape
        inner = w_out.shape[0]
        heads = a_neg.shape[0]
        tiles = inner // TILE
        segs = tokens // SEG
        assert mesh.shape["sp"] == 8 and heads == LANES and inner == heads * HEAD_DIM
        assert tiles >= LAG_Y + 2
        bc_at = 2 * inner // (2 * STATE)
        dt_at = (2 * inner + 2 * STATE) // heads

        def fixed(shape):
            return pl.BlockSpec(shape, lambda i: (0,) * len(shape), pipeline_mode=pl.Buffered(1))

        def whole(shape):
            return pl.BlockSpec(shape, lambda i: (0,) * len(shape))

        half = (tiles, STATE, HALF)
        sems = pltpu.SemaphoreType.DMA((tiles,))
        u, xw, bc, bt, gl, qt, dec, h_in = pl.pallas_call(
            project_kernel,
            grid=(2 * tiles,),
            out_shape=[
                jax.ShapeDtypeStruct((tokens, 2 * inner), BF16),
                jax.ShapeDtypeStruct((tokens, inner), BF16),
                jax.ShapeDtypeStruct((tokens, 2 * STATE), BF16),
                jax.ShapeDtypeStruct((segs * STATE, SEG), BF16),
                jax.ShapeDtypeStruct((tokens, heads), F32),
                jax.ShapeDtypeStruct((segs * heads, SEG), F32),
                jax.ShapeDtypeStruct((8, heads), F32),
                jax.ShapeDtypeStruct((STATE, inner), F32),
            ],
            in_specs=[
                fixed((tokens, d_model)),
                pl.BlockSpec((d_model, TILE), lambda i: (0, lax.rem(i + tiles, 2 * tiles))),
                pl.BlockSpec((d_model, 2 * STATE), lambda i: (0, bc_at), pipeline_mode=pl.Buffered(1)),
                pl.BlockSpec((d_model, heads), lambda i: (0, dt_at), pipeline_mode=pl.Buffered(1)),
                fixed((1, heads)), fixed((1, heads)),
            ],
            out_specs=[
                pl.BlockSpec((tokens, TILE), lambda i: (0, lax.rem(i + tiles, 2 * tiles))),
                pl.BlockSpec((tokens, TILE), lambda i: (0, jnp.minimum(i, tiles - 1))),
                whole((tokens, 2 * STATE)), whole((segs * STATE, SEG)), whole((tokens, heads)),
                whole((segs * heads, SEG)), whole((8, heads)),
                pl.BlockSpec((STATE, TILE), lambda i: (0, jnp.maximum(i - (LAG_Y + 2), 0))),
            ],
            scratch_shapes=[
                pltpu.VMEM((tokens, heads), F32),
                pltpu.VMEM((8, heads), F32),
                pltpu.VMEM((8, 8, heads), F32),
                pltpu.VMEM((tiles, 2, STATE, HALF), F32),
                pltpu.VMEM(half, F32), pltpu.VMEM(half, F32), pltpu.VMEM(half, F32),
                pltpu.VMEM(half, F32), pltpu.VMEM(half, F32), pltpu.VMEM(half, F32),
                pltpu.SemaphoreType.DMA((7,)), pltpu.SemaphoreType.DMA((8,)),
                sems, sems, sems, sems, sems, sems, sems, sems,
            ],
            compiler_params=pltpu.CompilerParams(
                dimension_semantics=("arbitrary",), collective_id=0, has_side_effects=True,
                vmem_limit_bytes=60 * 1024 * 1024),
            cost_estimate=pl.CostEstimate(flops=2 * tokens * d_model * w_in.shape[1],
                                          bytes_accessed=2 * w_in.size, transcendentals=0),
            name="project",
        )(x_loc, w_in, w_in, w_in, a_neg.reshape(1, heads), dt_bias.reshape(1, heads))

        return pl.pallas_call(
            mix_kernel,
            grid=(tiles,),
            out_shape=jax.ShapeDtypeStruct((tokens, d_model), BF16),
            in_specs=[
                pl.BlockSpec((tokens, TILE), lambda i: (0, i)),
                pl.BlockSpec((tokens, TILE), lambda i: (0, i + tiles)),
                pl.BlockSpec((tokens, TILE), lambda i: (0, i)),
                pl.BlockSpec((STATE, TILE), lambda i: (0, i)),
                fixed((tokens, 2 * STATE)), fixed((segs * STATE, SEG)), fixed((tokens, heads)),
                fixed((segs * heads, SEG)), fixed((8, heads)), fixed((1, heads)),
                fixed((tokens, d_model)),
                pl.BlockSpec((TILE, d_model), lambda i: (i, 0)),
            ],
            out_specs=pl.BlockSpec((tokens, d_model), lambda i: (0, 0)),
            scratch_shapes=[
                pltpu.VMEM((tokens, d_model), F32),
                pltpu.VMEM((tokens, TILE), BF16),
                pltpu.VMEM((tokens, SEG), F32),
            ],
            compiler_params=pltpu.CompilerParams(
                dimension_semantics=("arbitrary",), vmem_limit_bytes=60 * 1024 * 1024),
            cost_estimate=pl.CostEstimate(flops=2 * tokens * d_model * inner,
                                          bytes_accessed=2 * w_out.size, transcendentals=0),
            name="mix",
        )(u, u, xw, h_in, bc, bt, gl, qt, dec, d_skip.reshape(1, heads), x_loc, w_out)

    return jax.shard_map(local_mixer, mesh=mesh, in_specs=(row_spec, P(), P(), P(), P(), P()),
                         out_specs=row_spec, check_vma=False)
```

profile of v0, /device:TPU:0, one launch (start us, length us, event | category | flops | bytes accessed | tf_op | source)
XLA Modules:
  0.0 190.1 jit_solution(3224507382262632793)
XLA Ops:
  0.0 119.3 %project.1 = (bf16[512,16384]{1,0:T(8,128)(2,1)}, bf16[512,8192]{1,0:T(8,128)(2,1)}, bf16[512,256]{1,0:T(8,128)(2,1)}, bf16[512,128]{1,0:T(8,128)(2,1)}, f32[512...) custom-call(bf16[512,4096]{1,0:T(8,128)(2,1)} %x_ref.3, ...), custom_call_target="tpu_custom_call" | custom-call | flops 70330089472 | bytes 137363456 | tf_op jit(solution)/shard_map/project/pallas_call | solution.py:280
  119.4 70.8 %mix.1 = bf16[512,4096]{1,0:T(8,128)(2,1)} custom-call(bf16[512,16384]{1,0:T(8,128)(2,1)} %get-tuple-element.13.z_ref.xs_ref, bf16[512,16384]{1,0:T(8,128)(2,1)} %get-tuple-element.13.z_ref.xs_ref, bf16[512,8192]{1,0:T(8,128)(2,1)} %get-tuple-element.14.xw_ref, f32[128,8192]{1,0:T(8,128)} %get-tuple-element.15.h_ref, ...), custom_call_target="tpu_custom_call" | custom-call | flops 34359738368 | bytes 67108864 | tf_op jit(solution)/shard_map/mix/pallas_call | solution.py:325
where the time goes:
time: 190 us
  Pallas kernels  190 us (100%)
    pallas_call x1, Pallas kernels, local_mixer(): pl.pallas_call(project_kernel, grid=(2 * tiles,), out_shape=[jax.ShapeDty...  119 us
    pallas_call x1, Pallas kernels, local_mixer(): pl.pallas_call(mix_kernel, grid=(tiles,), out_shape=jax.ShapeDtypeStruct(...  70.8 us

commit v1 on v0

--- a/solution.py
+++ b/solution.py
@@ -12,7 +12,7 @@
 HALF = TILE // 2
 TILE_HEADS = TILE // HEAD_DIM
 LANES = 128
-LAG_X = 8
+LAG_X = 9
 LAG_Y = 14
 LOG2E = 1.4426950408889634
 MESH = pl.DeviceIdType.MESH
@@ -41,7 +41,7 @@
 
 def project_kernel(x_ref, w_ref, wbc_ref, wdt_ref, an_ref, db_ref,
                    u_ref, xw_ref, bc_ref, bt_ref, gl_ref, qt_ref, dec_ref, hin_ref,
-                   wst, lsend, lall, s_own, rc, sx, rx, sy, ry, rf,
+                   wst, uprev, drow, lsend, lall, s_own, rc, sx, rx, sy, ry, rf,
                    lsem, lrem, csem, crem, xsem, xrem, ysem, yrem, fsem, frem):
     step = pl.program_id(0)
     me = lax.axis_index("sp")
@@ -84,9 +84,30 @@
     def at_lag(lag):
         return jnp.logical_and(step >= lag, step < tiles + lag)
 
-    def decay_row(logs, c):
-        first = c * TILE_HEADS + core * (TILE_HEADS // 2)
-        return spread(lane_shift(jnp.exp(logs), first), 2)[:1]
+    def state_half(h, tile):
+        cols = slice(h * HALF, (h + 1) * HALF)
+        first = tile * TILE_HEADS + h * (TILE_HEADS // 2)
+        weights = lane_shift(wst[...], first)
+        dec = spread(lane_shift(dec_ref[...], first), 2)
+        parts = []
+        for c in range(segs):
+            rows = slice(c * SEG, (c + 1) * SEG)
+            xw = (uprev[rows, cols].astype(F32) * spread(weights[rows], 2)).astype(BF16)
+            xw_ref[rows, cols] = xw
+            parts.append(xw)
+
+        def finish():
+            state = dot32(bt_ref[:SEG, :], parts[0])
+            for c in range(1, segs):
+                state = dec[c:c + 1] * state + dot32(bt_ref[c * SEG:(c + 1) * SEG, :], parts[c])
+            s_own[tile, h] = state
+        return finish
+
+    def project_half(h):
+        cols = slice(h * HALF, (h + 1) * HALF)
+        u = dot32(x_ref[...], w_ref[:, cols]).astype(BF16)
+        u_ref[:, cols] = u
+        uprev[:, cols] = u
 
     @pl.when(step == 0)
     def _():
@@ -116,6 +137,9 @@
         dec_ref[...] = dec
         lsend[...] = jnp.broadcast_to(total, (8, LANES))
 
+    def s_of(mine, c):
+        return jnp.where(mine, s_own[c, core], rc[c])
+
     @pl.when(step == 1)
     def _():
         pl.semaphore_wait(barrier, 7)
@@ -123,9 +147,9 @@
             log_copy(k).start()
         lall[me] = lsend[...]
 
-    @pl.when(at_lag(1))
-    def _():
-        core_copy(step - 1).start()
+    @pl.when(at_lag(2))
+    def _():
+        core_copy(step - 2).start()
 
     @pl.when(step == 2)
     def _():
@@ -135,19 +159,25 @@
             pltpu.make_async_remote_copy(
                 src_ref=lsend, dst_ref=lall.at[source], send_sem=lsem.at[k - 1], recv_sem=lrem.at[source],
                 device_id={"sp": source}, device_id_type=MESH).wait_recv()
-
-    @pl.when(at_lag(2))
-    def _():
-        c = step - 2
+        chip = ypos * 4
+        row = lax.broadcasted_iota(jnp.int32, (8, LANES), 0)
+        logs = jnp.where(row == 0, lall[me - core + 1], 0.0)
+        logs = jnp.where(row == 1, lall[chip + 2] + lall[chip + 3], logs)
+        logs = jnp.where(jnp.logical_and(row == 2, xpos == 1), lall[chip] + lall[chip + 1], logs)
+        logs = jnp.where(row == 3, lall[me - core], logs)
+        decays = jnp.exp(logs)
+        for c in range(tiles):
+            drow[c] = spread(lane_shift(decays, c * TILE_HEADS + core * (TILE_HEADS // 2)), 2)
+
+    @pl.when(at_lag(3))
+    def _():
+        c = step - 3
         core_copy(c).wait()
-        mine, got = s_own[c, core], rc[c]
-        early = jnp.where(core == 0, mine, got)
-        late = jnp.where(core == 0, got, mine)
-        sx[c] = decay_row(lall[me - core + 1], c) * early + late
-
-    @pl.when(at_lag(3))
-    def _():
-        x_copy(step - 3).start()
+        sx[c] = drow[c, 0:1] * s_of(core == 0, c) + s_of(core == 1, c)
+
+    @pl.when(at_lag(4))
+    def _():
+        x_copy(step - 4).start()
 
     @pl.when(at_lag(LAG_X))
     def _():
@@ -156,8 +186,7 @@
         mine, got = sx[c], rx[c]
         early = jnp.where(xpos == 0, mine, got)
         late = jnp.where(xpos == 0, got, mine)
-        chip = ypos * 4 + 2
-        sy[c] = decay_row(lall[chip] + lall[chip + 1], c) * early + late
+        sy[c] = drow[c, 1:2] * early + late
 
     @pl.when(at_lag(LAG_X + 1))
     def _():
@@ -167,11 +196,8 @@
     def _():
         c = step - LAG_Y
         y_copy(c).wait()
-        chip = ypos * 4
-        logs = jnp.where(xpos == 1, lall[chip] + lall[chip + 1], 0.0)
-        before = jnp.where(xpos == 1, rx[c], 0.0) + jnp.where(ypos == 1, decay_row(logs, c) * ry[c], 0.0)
-        first = jnp.where(core == 0, s_own[c, core], rc[c])
-        after = decay_row(lall[me - core], c) * before + first
+        before = jnp.where(xpos == 1, rx[c], 0.0) + jnp.where(ypos == 1, drow[c, 2:3] * ry[c], 0.0)
+        after = drow[c, 3:4] * before + s_of(core == 0, c)
         sx[c] = jnp.where(core == 0, before, after)
         sy[c] = jnp.where(core == 0, after, before)
 
@@ -187,72 +213,103 @@
         hin_ref[:, :HALF] = jnp.where(core == 0, mine, got)
         hin_ref[:, HALF:] = jnp.where(core == 0, got, mine)
 
-    u = dot32(x_ref[...], w_ref[...]).astype(BF16)
-    u_ref[...] = u
-
-    @pl.when(step < tiles)
-    def _():
-        weights = lane_shift(wst[...], step * TILE_HEADS)
-        dec = spread(lane_shift(dec_ref[...], step * TILE_HEADS), TILE_HEADS // 2)
-        state = jnp.zeros((STATE, TILE), F32)
+    with_state = jnp.logical_and(step >= 1, step <= tiles)
+
+    @pl.when(with_state)
+    def _():
+        for h in range(2):
+            finish = state_half(h, step - 1)
+            project_half(h)
+            finish()
+
+    @pl.when(jnp.logical_not(with_state))
+    def _():
+        for h in range(2):
+            project_half(h)
+
+
+def mix_kernel(z_ref, xs_ref, xw_ref, h_ref, bc_ref, bt_ref, gl_ref, qt_ref, dec_ref, ds_ref, wa_ref, wb_ref, x_hbm,
+               out_ref, acc, gated_a, gated_b, scores, x_res, x_sem):
+    step = pl.program_id(0)
+    steps = pl.num_programs(0)
+    tokens, d_model = acc.shape
+    segs = tokens // SEG
+    x_copy = pltpu.make_async_copy(x_hbm, x_res, x_sem)
+
+    def dot_slice(k, source, w_ref):
+        cols = slice(k * TILE, (k + 1) * TILE)
+        acc[:, cols] += dot32(source[...], w_ref[:, cols])
+
+    def group_outputs(half, target, big):
+        base = half * TILE
+        first = (2 * step + half) * TILE_HEADS
+        gl = lane_shift(gl_ref[...], first)
+        dec = spread(lane_shift(dec_ref[...], first), TILE_HEADS // 2)
+        skip = spread(lane_shift(jnp.broadcast_to(ds_ref[...], (8, LANES)), first), TILE_HEADS // 2)[:1]
+        causal = (lax.broadcasted_iota(jnp.int32, (SEG, SEG), 0)
+                  >= lax.broadcasted_iota(jnp.int32, (SEG, SEG), 1))
+        low = lax.broadcasted_iota(jnp.int32, (SEG, LANES), 1) < HEAD_DIM
+        zero = jnp.zeros((SEG, LANES), BF16)
+        state = h_ref[:, base:base + TILE]
+        pending = None
+        unit = 0
         for c in range(segs):
             rows = slice(c * SEG, (c + 1) * SEG)
-            xw = (u_ref[rows, :].astype(F32) * spread(weights[rows], TILE_HEADS // 2)).astype(BF16)
-            xw_ref[rows, :] = xw
-            state = dec[c:c + 1] * state + dot32(bt_ref[rows, :], xw)
-        s_own[step, 0] = state[:, :HALF]
-        s_own[step, 1] = state[:, HALF:]
-
-
-def mix_kernel(z_ref, xs_ref, xw_ref, h_ref, bc_ref, bt_ref, gl_ref, qt_ref, dec_ref, ds_ref, x_ref, wo_ref,
-               out_ref, acc, gated, scores):
-    group = pl.program_id(0)
-    groups = pl.num_programs(0)
-    tokens = x_ref.shape[0]
-    segs = tokens // SEG
-
-    @pl.when(group == 0)
-    def _():
-        acc[...] = x_ref[...].astype(F32)
+            y_state = dot32(bc_ref[rows, STATE:], state.astype(BF16))
+            if c < segs - 1:
+                grown = dot32(bt_ref[rows, :], xw_ref[rows, base:base + TILE])
+            q_rows = qt_ref[pl.ds(pl.multiple_of(c * SEG + first, TILE_HEADS), TILE_HEADS), :]
+            for p in range(TILE_HEADS // 2):
+                cols = slice(base + p * LANES, base + (p + 1) * LANES)
+                sc = scores[rows, :]
+                col_a = jnp.broadcast_to(gl[rows, 2 * p:2 * p + 1], (SEG, LANES))
+                col_b = jnp.broadcast_to(gl[rows, 2 * p + 1:2 * p + 2], (SEG, LANES))
+                g_a = jnp.where(causal, sc * jnp.exp2(col_a - q_rows[2 * p:2 * p + 1]), 0.0).astype(BF16)
+                g_b = jnp.where(causal, sc * jnp.exp2(col_b - q_rows[2 * p + 1:2 * p + 2]), 0.0).astype(BF16)
+                xp = xs_ref[rows, cols]
+                rhs = jnp.concatenate([jnp.where(low, xp, zero), jnp.where(low, zero, xp)], axis=0)
+                if unit % 2 == 0 and big is not None:
+                    dot_slice(unit // 2, *big)
+                y = dot32(jnp.concatenate([g_a, g_b], axis=1), rhs)
+                if pending is not None:
+                    pending()
+
+                def pending(y=y, rows=rows, cols=cols, p=p, y_state=y_state, col_a=col_a, col_b=col_b):
+                    here = slice(p * LANES, (p + 1) * LANES)
+                    total = y + y_state[:, here] * jnp.exp2(jnp.where(low, col_a, col_b))
+                    total = total + skip[:, here] * xs_ref[rows, cols].astype(F32)
+                    z = z_ref[rows, cols].astype(F32)
+                    target[rows, here] = (total * (z / (1.0 + jnp.exp(-z)))).astype(BF16)
+                unit += 1
+            if c < segs - 1:
+                state = dec[c:c + 1] * state + grown
+        pending()
+
+    @pl.when(step == 0)
+    def _():
+        x_copy.start()
+        acc[...] = jnp.zeros_like(acc)
         for c in range(segs):
             rows = slice(c * SEG, (c + 1) * SEG)
             scores[rows, :] = lax.dot_general(bc_ref[rows, STATE:], bc_ref[rows, :STATE],
                                               (((1,), (1,)), ((), ())), preferred_element_type=F32)
-
-    first = group * TILE_HEADS
-    gl = lane_shift(gl_ref[...], first)
-    dec = spread(lane_shift(dec_ref[...], first), TILE_HEADS // 2)
-    skip = spread(lane_shift(jnp.broadcast_to(ds_ref[...], (8, LANES)), first), TILE_HEADS // 2)[:1]
-    causal = (lax.broadcasted_iota(jnp.int32, (SEG, SEG), 0)
-              >= lax.broadcasted_iota(jnp.int32, (SEG, SEG), 1))
-    low = lax.broadcasted_iota(jnp.int32, (SEG, LANES), 1) < HEAD_DIM
-    zero = jnp.zeros((SEG, LANES), BF16)
-    state = h_ref[...]
-    for c in range(segs):
-        rows = slice(c * SEG, (c + 1) * SEG)
-        y_state = dot32(bc_ref[rows, STATE:], state.astype(BF16))
-        if c < segs - 1:
-            state = dec[c:c + 1] * state + dot32(bt_ref[rows, :], xw_ref[rows, :])
-        q_rows = qt_ref[pl.ds(pl.multiple_of(c * SEG + first, TILE_HEADS), TILE_HEADS), :]
-        sc = scores[rows, :]
-        for p in range(TILE_HEADS // 2):
-            cols = slice(p * LANES, (p + 1) * LANES)
-            col_a = jnp.broadcast_to(gl[rows, 2 * p:2 * p + 1], (SEG, LANES))
-            col_b = jnp.broadcast_to(gl[rows, 2 * p + 1:2 * p + 2], (SEG, LANES))
-            g_a = jnp.where(causal, sc * jnp.exp2(col_a - q_rows[2 * p:2 * p + 1]), 0.0).astype(BF16)
-            g_b = jnp.where(causal, sc * jnp.exp2(col_b - q_rows[2 * p + 1:2 * p + 2]), 0.0).astype(BF16)
-            xp = xs_ref[rows, cols]
-            rhs = jnp.concatenate([jnp.where(low, xp, zero), jnp.where(low, zero, xp)], axis=0)
-            y = dot32(jnp.concatenate([g_a, g_b], axis=1), rhs)
-            y = y + y_state[:, cols] * jnp.exp2(jnp.where(low, col_a, col_b)) + skip[:, cols] * xp.astype(F32)
-            z = z_ref[rows, cols].astype(F32)
-            gated[rows, cols] = (y * (z / (1.0 + jnp.exp(-z)))).astype(BF16)
-
-    acc[...] += dot32(gated[...], wo_ref[...])
-
-    @pl.when(group == groups - 1)
-    def _():
-        out_ref[...] = acc[...].astype(BF16)
+        group_outputs(0, gated_a, None)
+
+    @pl.when(jnp.logical_and(step > 0, step < steps - 1))
+    def _():
+        group_outputs(0, gated_a, (gated_b, wa_ref))
+
+    @pl.when(step < steps - 1)
+    def _():
+        group_outputs(1, gated_b, (gated_a, wb_ref))
+
+    @pl.when(step == steps - 1)
+    def _():
+        x_copy.wait()
+        for k in range(d_model // TILE):
+            cols = slice(k * TILE, (k + 1) * TILE)
+            total = acc[:, cols] + dot32(gated_b[...], wa_ref[:, cols])
+            out_ref[:, cols] = (x_res[:, cols].astype(F32) + total).astype(BF16)
 
 
 def solution(mesh):
@@ -299,13 +356,15 @@
             ],
             out_specs=[
                 pl.BlockSpec((tokens, TILE), lambda i: (0, lax.rem(i + tiles, 2 * tiles))),
-                pl.BlockSpec((tokens, TILE), lambda i: (0, jnp.minimum(i, tiles - 1))),
+                pl.BlockSpec((tokens, TILE), lambda i: (0, jnp.clip(i - 1, 0, tiles - 1))),
                 whole((tokens, 2 * STATE)), whole((segs * STATE, SEG)), whole((tokens, heads)),
                 whole((segs * heads, SEG)), whole((8, heads)),
                 pl.BlockSpec((STATE, TILE), lambda i: (0, jnp.maximum(i - (LAG_Y + 2), 0))),
             ],
             scratch_shapes=[
                 pltpu.VMEM((tokens, heads), F32),
+                pltpu.VMEM((tokens, TILE), BF16),
+                pltpu.VMEM((tiles, 8, HALF), F32),
                 pltpu.VMEM((8, heads), F32),
                 pltpu.VMEM((8, 8, heads), F32),
                 pltpu.VMEM((tiles, 2, STATE, HALF), F32),
@@ -322,32 +381,37 @@
             name="project",
         )(x_loc, w_in, w_in, w_in, a_neg.reshape(1, heads), dt_bias.reshape(1, heads))
 
+        last = tiles // 2 - 1
         return pl.pallas_call(
             mix_kernel,
-            grid=(tiles,),
+            grid=(tiles // 2 + 1,),
             out_shape=jax.ShapeDtypeStruct((tokens, d_model), BF16),
             in_specs=[
-                pl.BlockSpec((tokens, TILE), lambda i: (0, i)),
-                pl.BlockSpec((tokens, TILE), lambda i: (0, i + tiles)),
-                pl.BlockSpec((tokens, TILE), lambda i: (0, i)),
-                pl.BlockSpec((STATE, TILE), lambda i: (0, i)),
+                pl.BlockSpec((tokens, 2 * TILE), lambda i: (0, jnp.minimum(i, last))),
+                pl.BlockSpec((tokens, 2 * TILE), lambda i: (0, jnp.minimum(i, last) + tiles // 2)),
+                pl.BlockSpec((tokens, 2 * TILE), lambda i: (0, jnp.minimum(i, last))),
+                pl.BlockSpec((STATE, 2 * TILE), lambda i: (0, jnp.minimum(i, last))),
                 fixed((tokens, 2 * STATE)), fixed((segs * STATE, SEG)), fixed((tokens, heads)),
                 fixed((segs * heads, SEG)), fixed((8, heads)), fixed((1, heads)),
-                fixed((tokens, d_model)),
-                pl.BlockSpec((TILE, d_model), lambda i: (i, 0)),
-            ],
-            out_specs=pl.BlockSpec((tokens, d_model), lambda i: (0, 0)),
+                pl.BlockSpec((TILE, d_model), lambda i: (jnp.maximum(2 * i - 1, 0), 0)),
+                pl.BlockSpec((TILE, d_model), lambda i: (jnp.minimum(2 * i, tiles - 2), 0)),
+                pl.BlockSpec(memory_space=pl.ANY),
+            ],
+            out_specs=pl.BlockSpec((tokens, d_model), lambda i: (0, 0), pipeline_mode=pl.Buffered(1)),
             scratch_shapes=[
                 pltpu.VMEM((tokens, d_model), F32),
                 pltpu.VMEM((tokens, TILE), BF16),
+                pltpu.VMEM((tokens, TILE), BF16),
                 pltpu.VMEM((tokens, SEG), F32),
+                pltpu.VMEM((tokens, d_model), BF16),
+                pltpu.SemaphoreType.DMA(()),
             ],
             compiler_params=pltpu.CompilerParams(
-                dimension_semantics=("arbitrary",), vmem_limit_bytes=60 * 1024 * 1024),
+                dimension_semantics=("arbitrary",), vmem_limit_bytes=62 * 1024 * 1024),
             cost_estimate=pl.CostEstimate(flops=2 * tokens * d_model * inner,
                                           bytes_accessed=2 * w_out.size, transcendentals=0),
             name="mix",
-        )(u, u, xw, h_in, bc, bt, gl, qt, dec, d_skip.reshape(1, heads), x_loc, w_out)
+        )(u, u, xw, h_in, bc, bt, gl, qt, dec, d_skip.reshape(1, heads), w_out, w_out, x_loc)
 
     return jax.shard_map(local_mixer, mesh=mesh, in_specs=(row_spec, P(), P(), P(), P(), P()),
                          out_specs=row_spec, check_vma=False)

time: 190 us -> 170 us (0.89)
  Pallas kernels: 190 us -> 169 us
    pallas_call x1, Pallas kernels: 119 us -> 108 us  [local_mixer(): pl.pallas_call(project_kernel, grid=(2 * tiles,), out_shape=[jax.ShapeDty...]
    pallas_call x1, Pallas kernels: 70.8 us -> 61.8 us  [local_mixer(): pl.pallas_call(mix_kernel, grid=(tiles // 2 + 1,), out_shape=jax.ShapeDty...]
where the time goes in v1:
time: 170 us; the launch traced here: 169 us
  Pallas kernels  169 us (99%)
    pallas_call x1, Pallas kernels, local_mixer(): pl.pallas_call(project_kernel, grid=(2 * tiles,), out_shape=[jax.ShapeDty...  108 us
    pallas_call x1, Pallas kernels, local_mixer(): pl.pallas_call(mix_kernel, grid=(tiles // 2 + 1,), out_shape=jax.ShapeDty...  61.8 us

profile of v1, /device:TPU:0, one launch (start us, length us, event | category | flops | bytes accessed | tf_op | source)
XLA Modules:
  0.0 169.4 jit_solution(15034256049370182833)
XLA Ops:
  0.0 107.5 %project.1 = (bf16[512,16384]{1,0:T(8,128)(2,1)}, bf16[512,8192]{1,0:T(8,128)(2,1)}, bf16[512,256]{1,0:T(8,128)(2,1)}, bf16[512,128]{1,0:T(8,128)(2,1)}, f32[512...) custom-call(bf16[512,4096]{1,0:T(8,128)(2,1)} %x_hbm.1, ...), custom_call_target="tpu_custom_call" | custom-call | flops 70330089472 | bytes 137363456 | tf_op jit(solution)/shard_map/project/pallas_call | solution.py:337
  107.5 61.8 %mix.1 = bf16[512,4096]{1,0:T(8,128)(2,1)} custom-call(bf16[512,16384]{1,0:T(8,128)(2,1)} %get-tuple-element.13.z_ref.xs_ref, bf16[512,16384]{1,0:T(8,128)(2,1)} %get-tuple-element.13.z_ref.xs_ref, bf16[512,8192]{1,0:T(8,128)(2,1)} %get-tuple-element.14.xw_ref, f32[128,8192]{1,0:T(8,128)} %get-tuple-element.15.h_ref, ...), custom_call_target="tpu_custom_call" | custom-call | flops 34359738368 | bytes 67108864 | tf_op jit(solution)/shard_map/mix/pallas_call | solution.py:385

commit v2 on v1

--- a/solution.py
+++ b/solution.py
@@ -39,15 +39,30 @@
     return pltpu.roll(v, lax.rem(LANES - first, LANES), 1)
 
 
-def project_kernel(x_ref, w_ref, wbc_ref, wdt_ref, an_ref, db_ref,
-                   u_ref, xw_ref, bc_ref, bt_ref, gl_ref, qt_ref, dec_ref, hin_ref,
-                   wst, uprev, drow, lsend, lall, s_own, rc, sx, rx, sy, ry, rf,
+def project_kernel(x_hbm, w_ref, w_hbm, an_hbm, db_hbm,
+                   u_ref, loc_ref, hin_ref, bc_hbm, gl_hbm, qt_hbm, dec_hbm,
+                   x_ref, wbc_ref, wdt_ref, an_ref, db_ref, bc_ref, gl_ref, qt_ref, dec_ref, isem, osem,
+                   bt_ref, seg_dec, xw_ref, wst, uprev, drow, lsend, lall, s_own, rc, sx, rx, sy, ry, rf,
                    lsem, lrem, csem, crem, xsem, xrem, ysem, yrem, fsem, frem):
     step = pl.program_id(0)
     me = lax.axis_index("sp")
     tokens = x_ref.shape[0]
     segs = tokens // SEG
     tiles = s_own.shape[0]
+    heads_at = 2 * tiles * TILE
+    loads = [
+        pltpu.make_async_copy(db_hbm, db_ref, isem.at[0]),
+        pltpu.make_async_copy(an_hbm, an_ref, isem.at[1]),
+        pltpu.make_async_copy(w_hbm.at[:, heads_at + 2 * STATE:], wdt_ref, isem.at[2]),
+        pltpu.make_async_copy(x_hbm, x_ref, isem.at[3]),
+        pltpu.make_async_copy(w_hbm.at[:, heads_at:heads_at + 2 * STATE], wbc_ref, isem.at[4]),
+    ]
+    stores = [
+        pltpu.make_async_copy(bc_ref, bc_hbm, osem.at[0]),
+        pltpu.make_async_copy(gl_ref, gl_hbm, osem.at[1]),
+        pltpu.make_async_copy(qt_ref, qt_hbm, osem.at[2]),
+        pltpu.make_async_copy(dec_ref, dec_hbm, osem.at[3]),
+    ]
     core = lax.rem(me, 2)
     xpos = lax.rem(me // 2, 2)
     ypos = me // 4
@@ -84,24 +99,22 @@
     def at_lag(lag):
         return jnp.logical_and(step >= lag, step < tiles + lag)
 
-    def state_half(h, tile):
-        cols = slice(h * HALF, (h + 1) * HALF)
-        first = tile * TILE_HEADS + h * (TILE_HEADS // 2)
-        weights = lane_shift(wst[...], first)
-        dec = spread(lane_shift(dec_ref[...], first), 2)
-        parts = []
+    def weigh(tile):
+        weights = lane_shift(wst[...], tile * TILE_HEADS)
         for c in range(segs):
             rows = slice(c * SEG, (c + 1) * SEG)
-            xw = (uprev[rows, cols].astype(F32) * spread(weights[rows], 2)).astype(BF16)
-            xw_ref[rows, cols] = xw
-            parts.append(xw)
-
-        def finish():
-            state = dot32(bt_ref[:SEG, :], parts[0])
-            for c in range(1, segs):
-                state = dec[c:c + 1] * state + dot32(bt_ref[c * SEG:(c + 1) * SEG, :], parts[c])
-            s_own[tile, h] = state
-        return finish
+            spread_rows = spread(weights[rows], TILE_HEADS // 2)
+            xw_ref[rows, :] = (uprev[rows, :].astype(F32) * spread_rows).astype(BF16)
+
+    def states(tile):
+        dec = spread(lane_shift(seg_dec[...], tile * TILE_HEADS), TILE_HEADS // 2)
+        state = dot32(bt_ref[:SEG, :], xw_ref[:SEG, :])
+        for c in range(1, segs):
+            rows = slice(c * SEG, (c + 1) * SEG)
+            loc_ref[(c - 1) * STATE:c * STATE, :] = state
+            state = dec[c:c + 1] * state + dot32(bt_ref[rows, :], xw_ref[rows, :])
+        s_own[tile, 0] = state[:, :HALF]
+        s_own[tile, 1] = state[:, HALF:]
 
     def project_half(h):
         cols = slice(h * HALF, (h + 1) * HALF)
@@ -113,10 +126,14 @@
     def _():
         for k in range(1, 8):
             pl.semaphore_signal(barrier, inc=1, device_id={"sp": other(k)}, device_id_type=MESH)
-        x = x_ref[...]
-        bc = dot32(x, wbc_ref[...]).astype(BF16)
+        for load in loads:
+            load.start()
+        for load in loads[:4]:
+            load.wait()
+        raw = dot32(x_ref[...], wdt_ref[...]).astype(BF16).astype(F32) + db_ref[...]
+        loads[4].wait()
+        bc = dot32(x_ref[...], wbc_ref[...]).astype(BF16)
         bc_ref[...] = bc
-        raw = dot32(x, wdt_ref[...]).astype(BF16).astype(F32) + db_ref[...]
         dt = jnp.maximum(raw, 0.0) + jnp.log1p(jnp.exp(-jnp.abs(raw)))
         logs = dt * an_ref[...]
         tri = (lax.broadcasted_iota(jnp.int32, (SEG, SEG), 0)
@@ -124,6 +141,7 @@
         total = jnp.zeros((1, LANES), F32)
         row = lax.broadcasted_iota(jnp.int32, (8, LANES), 0)
         dec = jnp.zeros((8, LANES), F32)
+        before = jnp.zeros((8, LANES), F32)
         for c in range(segs):
             rows = slice(c * SEG, (c + 1) * SEG)
             cum = jnp.dot(tri, logs[rows], precision=lax.Precision.HIGHEST, preferred_element_type=F32)
@@ -133,8 +151,10 @@
             qt_ref[rows, :] = jnp.transpose(cum * LOG2E - jnp.log2(dt[rows]))
             bt_ref[rows, :] = jnp.transpose(bc[rows, :STATE].astype(F32)).astype(BF16)
             dec = jnp.where(row == c, jnp.exp(last), dec)
+            before = jnp.where(row == c, jnp.exp(total), before)
             total = total + last
-        dec_ref[...] = dec
+        seg_dec[...] = dec
+        dec_ref[...] = before
         lsend[...] = jnp.broadcast_to(total, (8, LANES))
 
     def s_of(mine, c):
@@ -143,6 +163,8 @@
     @pl.when(step == 1)
     def _():
         pl.semaphore_wait(barrier, 7)
+        for store in stores:
+            store.start()
         for k in range(1, 8):
             log_copy(k).start()
         lall[me] = lsend[...]
@@ -217,28 +239,45 @@
 
     @pl.when(with_state)
     def _():
-        for h in range(2):
-            finish = state_half(h, step - 1)
-            project_half(h)
-            finish()
+        weigh(step - 1)
+        project_half(0)
+        states(step - 1)
+        project_half(1)
 
     @pl.when(jnp.logical_not(with_state))
     def _():
         for h in range(2):
             project_half(h)
 
-
-def mix_kernel(z_ref, xs_ref, xw_ref, h_ref, bc_ref, bt_ref, gl_ref, qt_ref, dec_ref, ds_ref, wa_ref, wb_ref, x_hbm,
-               out_ref, acc, gated_a, gated_b, scores, x_res, x_sem):
+    @pl.when(step == 2 * tiles - 1)
+    def _():
+        for store in stores:
+            store.wait()
+
+
+def mix_kernel(z_ref, xs_ref, loc_ref, h_ref, bc_ref, gl_ref, qt_ref, dec_ref, ds_ref, w_hbm, x_hbm,
+               out_hbm, acc, gated_a, gated_b, scores, wbuf, out_ref, w_sem, x_sem, o_sem):
     step = pl.program_id(0)
     steps = pl.num_programs(0)
     tokens, d_model = acc.shape
     segs = tokens // SEG
-    x_copy = pltpu.make_async_copy(x_hbm, x_res, x_sem)
-
-    def dot_slice(k, source, w_ref):
+    slots = wbuf.shape[0]
+    groups = w_hbm.shape[0] // TILE
+    x_copy = pltpu.make_async_copy(x_hbm, out_ref, x_sem)
+
+    def w_copy(group):
+        slot = lax.rem(group, slots)
+        first = pl.multiple_of(group * TILE, TILE)
+        return pltpu.make_async_copy(w_hbm.at[pl.ds(first, TILE), :], wbuf.at[slot], w_sem.at[slot])
+
+    def w_next(group):
+        @pl.when(group + slots < groups)
+        def _():
+            w_copy(group + slots).start()
+
+    def dot_slice(k, source, group):
         cols = slice(k * TILE, (k + 1) * TILE)
-        acc[:, cols] += dot32(source[...], w_ref[:, cols])
+        acc[:, cols] += dot32(source[...], wbuf[lax.rem(group, slots), :, cols])
 
     def group_outputs(half, target, big):
         base = half * TILE
@@ -250,14 +289,14 @@
                   >= lax.broadcasted_iota(jnp.int32, (SEG, SEG), 1))
         low = lax.broadcasted_iota(jnp.int32, (SEG, LANES), 1) < HEAD_DIM
         zero = jnp.zeros((SEG, LANES), BF16)
-        state = h_ref[:, base:base + TILE]
         pending = None
         unit = 0
         for c in range(segs):
             rows = slice(c * SEG, (c + 1) * SEG)
+            state = h_ref[:, base:base + TILE]
+            if c > 0:
+                state = dec[c:c + 1] * state + loc_ref[(c - 1) * STATE:c * STATE, base:base + TILE]
             y_state = dot32(bc_ref[rows, STATE:], state.astype(BF16))
-            if c < segs - 1:
-                grown = dot32(bt_ref[rows, :], xw_ref[rows, base:base + TILE])
             q_rows = qt_ref[pl.ds(pl.multiple_of(c * SEG + first, TILE_HEADS), TILE_HEADS), :]
             for p in range(TILE_HEADS // 2):
                 cols = slice(base + p * LANES, base + (p + 1) * LANES)
@@ -281,12 +320,12 @@
                     z = z_ref[rows, cols].astype(F32)
                     target[rows, here] = (total * (z / (1.0 + jnp.exp(-z)))).astype(BF16)
                 unit += 1
-            if c < segs - 1:
-                state = dec[c:c + 1] * state + grown
         pending()
 
     @pl.when(step == 0)
     def _():
+        for group in range(slots):
+            w_copy(group).start()
         x_copy.start()
         acc[...] = jnp.zeros_like(acc)
         for c in range(segs):
@@ -297,19 +336,29 @@
 
     @pl.when(jnp.logical_and(step > 0, step < steps - 1))
     def _():
-        group_outputs(0, gated_a, (gated_b, wa_ref))
+        w_copy(2 * step - 1).wait()
+        group_outputs(0, gated_a, (gated_b, 2 * step - 1))
+        w_next(2 * step - 1)
 
     @pl.when(step < steps - 1)
     def _():
-        group_outputs(1, gated_b, (gated_a, wb_ref))
+        w_copy(2 * step).wait()
+        group_outputs(1, gated_b, (gated_a, 2 * step))
+        w_next(2 * step)
 
     @pl.when(step == steps - 1)
     def _():
         x_copy.wait()
-        for k in range(d_model // TILE):
-            cols = slice(k * TILE, (k + 1) * TILE)
-            total = acc[:, cols] + dot32(gated_b[...], wa_ref[:, cols])
-            out_ref[:, cols] = (x_res[:, cols].astype(F32) + total).astype(BF16)
+        w_copy(groups - 1).wait()
+        copies = []
+        for k in range(d_model // (2 * TILE)):
+            cols = slice(2 * k * TILE, 2 * (k + 1) * TILE)
+            total = acc[:, cols] + dot32(gated_b[...], wbuf[(groups - 1) % slots, :, cols])
+            out_ref[:, cols] = (out_ref[:, cols].astype(F32) + total).astype(BF16)
+            copies.append(pltpu.make_async_copy(out_ref.at[:, cols], out_hbm.at[:, cols], o_sem.at[k]))
+            copies[-1].start()
+        for copy in copies:
+            copy.wait()
 
 
 def solution(mesh):
@@ -323,45 +372,48 @@
         segs = tokens // SEG
         assert mesh.shape["sp"] == 8 and heads == LANES and inner == heads * HEAD_DIM
         assert tiles >= LAG_Y + 2
-        bc_at = 2 * inner // (2 * STATE)
-        dt_at = (2 * inner + 2 * STATE) // heads
-
         def fixed(shape):
             return pl.BlockSpec(shape, lambda i: (0,) * len(shape), pipeline_mode=pl.Buffered(1))
 
-        def whole(shape):
-            return pl.BlockSpec(shape, lambda i: (0,) * len(shape))
-
         half = (tiles, STATE, HALF)
         sems = pltpu.SemaphoreType.DMA((tiles,))
-        u, xw, bc, bt, gl, qt, dec, h_in = pl.pallas_call(
+        any_space = pl.BlockSpec(memory_space=pl.ANY)
+        u, loc, h_in, bc, gl, qt, dec = pl.pallas_call(
             project_kernel,
             grid=(2 * tiles,),
             out_shape=[
                 jax.ShapeDtypeStruct((tokens, 2 * inner), BF16),
-                jax.ShapeDtypeStruct((tokens, inner), BF16),
+                jax.ShapeDtypeStruct(((segs - 1) * STATE, inner), F32),
+                jax.ShapeDtypeStruct((STATE, inner), F32),
                 jax.ShapeDtypeStruct((tokens, 2 * STATE), BF16),
-                jax.ShapeDtypeStruct((segs * STATE, SEG), BF16),
                 jax.ShapeDtypeStruct((tokens, heads), F32),
                 jax.ShapeDtypeStruct((segs * heads, SEG), F32),
                 jax.ShapeDtypeStruct((8, heads), F32),
-                jax.ShapeDtypeStruct((STATE, inner), F32),
             ],
             in_specs=[
-                fixed((tokens, d_model)),
+                any_space,
                 pl.BlockSpec((d_model, TILE), lambda i: (0, lax.rem(i + tiles, 2 * tiles))),
-                pl.BlockSpec((d_model, 2 * STATE), lambda i: (0, bc_at), pipeline_mode=pl.Buffered(1)),
-                pl.BlockSpec((d_model, heads), lambda i: (0, dt_at), pipeline_mode=pl.Buffered(1)),
-                fixed((1, heads)), fixed((1, heads)),
+                any_space, any_space, any_space,
             ],
             out_specs=[
                 pl.BlockSpec((tokens, TILE), lambda i: (0, lax.rem(i + tiles, 2 * tiles))),
-                pl.BlockSpec((tokens, TILE), lambda i: (0, jnp.clip(i - 1, 0, tiles - 1))),
-                whole((tokens, 2 * STATE)), whole((segs * STATE, SEG)), whole((tokens, heads)),
-                whole((segs * heads, SEG)), whole((8, heads)),
+                pl.BlockSpec(((segs - 1) * STATE, TILE), lambda i: (0, jnp.clip(i - 1, 0, tiles - 1))),
                 pl.BlockSpec((STATE, TILE), lambda i: (0, jnp.maximum(i - (LAG_Y + 2), 0))),
+                any_space, any_space, any_space, any_space,
             ],
             scratch_shapes=[
+                pltpu.VMEM((tokens, d_model), BF16),
+                pltpu.VMEM((d_model, 2 * STATE), BF16),
+                pltpu.VMEM((d_model, heads), BF16),
+                pltpu.VMEM((1, heads), F32), pltpu.VMEM((1, heads), F32),
+                pltpu.VMEM((tokens, 2 * STATE), BF16),
+                pltpu.VMEM((tokens, heads), F32),
+                pltpu.VMEM((segs * heads, SEG), F32),
+                pltpu.VMEM((8, heads), F32),
+                pltpu.SemaphoreType.DMA((5,)), pltpu.SemaphoreType.DMA((4,)),
+                pltpu.VMEM((segs * STATE, SEG), BF16),
+                pltpu.VMEM((8, heads), F32),
+                pltpu.VMEM((tokens, TILE), BF16),
                 pltpu.VMEM((tokens, heads), F32),
                 pltpu.VMEM((tokens, TILE), BF16),
                 pltpu.VMEM((tiles, 8, HALF), F32),
@@ -379,7 +431,7 @@
             cost_estimate=pl.CostEstimate(flops=2 * tokens * d_model * w_in.shape[1],
                                           bytes_accessed=2 * w_in.size, transcendentals=0),
             name="project",
-        )(x_loc, w_in, w_in, w_in, a_neg.reshape(1, heads), dt_bias.reshape(1, heads))
+        )(x_loc, w_in, w_in, a_neg.reshape(1, heads), dt_bias.reshape(1, heads))
 
         last = tiles // 2 - 1
         return pl.pallas_call(
@@ -389,29 +441,30 @@
             in_specs=[
                 pl.BlockSpec((tokens, 2 * TILE), lambda i: (0, jnp.minimum(i, last))),
                 pl.BlockSpec((tokens, 2 * TILE), lambda i: (0, jnp.minimum(i, last) + tiles // 2)),
-                pl.BlockSpec((tokens, 2 * TILE), lambda i: (0, jnp.minimum(i, last))),
+                pl.BlockSpec(((segs - 1) * STATE, 2 * TILE), lambda i: (0, jnp.minimum(i, last))),
                 pl.BlockSpec((STATE, 2 * TILE), lambda i: (0, jnp.minimum(i, last))),
-                fixed((tokens, 2 * STATE)), fixed((segs * STATE, SEG)), fixed((tokens, heads)),
+                fixed((tokens, 2 * STATE)), fixed((tokens, heads)),
                 fixed((segs * heads, SEG)), fixed((8, heads)), fixed((1, heads)),
-                pl.BlockSpec((TILE, d_model), lambda i: (jnp.maximum(2 * i - 1, 0), 0)),
-                pl.BlockSpec((TILE, d_model), lambda i: (jnp.minimum(2 * i, tiles - 2), 0)),
-                pl.BlockSpec(memory_space=pl.ANY),
-            ],
-            out_specs=pl.BlockSpec((tokens, d_model), lambda i: (0, 0), pipeline_mode=pl.Buffered(1)),
+                any_space, any_space,
+            ],
+            out_specs=any_space,
             scratch_shapes=[
                 pltpu.VMEM((tokens, d_model), F32),
                 pltpu.VMEM((tokens, TILE), BF16),
                 pltpu.VMEM((tokens, TILE), BF16),
                 pltpu.VMEM((tokens, SEG), F32),
+                pltpu.VMEM((4, TILE, d_model), BF16),
                 pltpu.VMEM((tokens, d_model), BF16),
+                pltpu.SemaphoreType.DMA((4,)),
                 pltpu.SemaphoreType.DMA(()),
+                pltpu.SemaphoreType.DMA((d_model // (2 * TILE),)),
             ],
             compiler_params=pltpu.CompilerParams(
                 dimension_semantics=("arbitrary",), vmem_limit_bytes=62 * 1024 * 1024),
             cost_estimate=pl.CostEstimate(flops=2 * tokens * d_model * inner,
                                           bytes_accessed=2 * w_out.size, transcendentals=0),
             name="mix",
-        )(u, u, xw, h_in, bc, bt, gl, qt, dec, d_skip.reshape(1, heads), w_out, w_out, x_loc)
+        )(u, u, loc, h_in, bc, gl, qt, dec, d_skip.reshape(1, heads), w_out, x_loc)
 
     return jax.shard_map(local_mixer, mesh=mesh, in_specs=(row_spec, P(), P(), P(), P(), P()),
                          out_specs=row_spec, check_vma=False)

time: 170 us -> 167 us (0.982)
  Pallas kernels: 169 us -> 167 us
    pallas_call x1, Pallas kernels: 61.8 us -> 53.9 us  [local_mixer(): pl.pallas_call(mix_kernel, grid=(tiles // 2 + 1,), out_shape=jax.ShapeDty...]
    pallas_call x1, Pallas kernels: 108 us -> 113 us  [local_mixer(): pl.pallas_call(project_kernel, grid=(2 * tiles,), out_shape=[jax.ShapeDty...]
where the time goes in v2:
time: 167 us
  Pallas kernels  167 us (100%)
    pallas_call x1, Pallas kernels, local_mixer(): pl.pallas_call(project_kernel, grid=(2 * tiles,), out_shape=[jax.ShapeDty...  113 us
    pallas_call x1, Pallas kernels, local_mixer(): pl.pallas_call(mix_kernel, grid=(tiles // 2 + 1,), out_shape=jax.ShapeDty...  53.9 us

profile of v2, /device:TPU:0, one launch (start us, length us, event | category | flops | bytes accessed | tf_op | source)
XLA Modules:
  0.0 167.1 jit_solution(7663369179119237185)
XLA Ops:
  0.0 113.0 %project.1 = (bf16[512,16384]{1,0:T(8,128)(2,1)}, f32[384,8192]{1,0:T(8,128)}, f32[128,8192]{1,0:T(8,128)}, bf16[512,256]{1,0:T(8,128)(2,1)}, f32[512,128]{1,0:T...) custom-call(bf16[512,4096]{1,0:T(8,128)(2,1)} %x_hbm.3, bf16[4096,16768]{1,0:T(8,128)(2,1)} %w_hbm.2, ...), custom_call_target="tpu_custom_call" | custom-call | flops 70330089472 | bytes 137363456 | tf_op jit(solution)/shard_map/project/pallas_call | solution.py:381
  113.0 53.9 %mix.1 = bf16[512,4096]{1,0:T(8,128)(2,1)} custom-call(bf16[512,16384]{1,0:T(8,128)(2,1)} %get-tuple-element.12.z_ref.xs_ref, bf16[512,16384]{1,0:T(8,128)(2,1)} %get-tuple-element.12.z_ref.xs_ref, f32[384,8192]{1,0:T(8,128)} %get-tuple-element.13.loc_ref, f32[128,8192]{1,0:T(8,128)} %get-tuple-element.14.h_ref, bf16[512,256]{1,0:T(8,128)(2,1)} %get-tuple-element.15.bc_ref, ...), custom_call_target="tpu_custom_call" | custom-call | flops 34359738368 | bytes 67108864 | tf_op jit(solution)/shard_map/mix/pallas_call | solution.py:437

commit v3 on v2

--- a/solution.py
+++ b/solution.py
@@ -41,7 +41,7 @@
 
 def project_kernel(x_hbm, w_ref, w_hbm, an_hbm, db_hbm,
                    u_ref, loc_ref, hin_ref, bc_hbm, gl_hbm, qt_hbm, dec_hbm,
-                   x_ref, wbc_ref, wdt_ref, an_ref, db_ref, bc_ref, gl_ref, qt_ref, dec_ref, isem, osem,
+                   x_ref, wdt_ref, an_ref, db_ref, bc_ref, gl_ref, qt_ref, dec_ref, isem, osem,
                    bt_ref, seg_dec, xw_ref, wst, uprev, drow, lsend, lall, s_own, rc, sx, rx, sy, ry, rf,
                    lsem, lrem, csem, crem, xsem, xrem, ysem, yrem, fsem, frem):
     step = pl.program_id(0)
@@ -53,9 +53,8 @@
     loads = [
         pltpu.make_async_copy(db_hbm, db_ref, isem.at[0]),
         pltpu.make_async_copy(an_hbm, an_ref, isem.at[1]),
-        pltpu.make_async_copy(w_hbm.at[:, heads_at + 2 * STATE:], wdt_ref, isem.at[2]),
-        pltpu.make_async_copy(x_hbm, x_ref, isem.at[3]),
-        pltpu.make_async_copy(w_hbm.at[:, heads_at:heads_at + 2 * STATE], wbc_ref, isem.at[4]),
+        pltpu.make_async_copy(x_hbm, x_ref, isem.at[2]),
+        pltpu.make_async_copy(w_hbm.at[:, heads_at:], wdt_ref, isem.at[3]),
     ]
     stores = [
         pltpu.make_async_copy(bc_ref, bc_hbm, osem.at[0]),
@@ -116,11 +115,10 @@
         s_own[tile, 0] = state[:, :HALF]
         s_own[tile, 1] = state[:, HALF:]
 
-    def project_half(h):
-        cols = slice(h * HALF, (h + 1) * HALF)
-        u = dot32(x_ref[...], w_ref[:, cols]).astype(BF16)
-        u_ref[:, cols] = u
-        uprev[:, cols] = u
+    def project():
+        u = dot32(x_ref[...], w_ref[...]).astype(BF16)
+        u_ref[...] = u
+        uprev[...] = u
 
     @pl.when(step == 0)
     def _():
@@ -128,12 +126,12 @@
             pl.semaphore_signal(barrier, inc=1, device_id={"sp": other(k)}, device_id_type=MESH)
         for load in loads:
             load.start()
-        for load in loads[:4]:
+        for load in loads:
             load.wait()
-        raw = dot32(x_ref[...], wdt_ref[...]).astype(BF16).astype(F32) + db_ref[...]
-        loads[4].wait()
-        bc = dot32(x_ref[...], wbc_ref[...]).astype(BF16)
+        last_columns = dot32(x_ref[...], wdt_ref[...]).astype(BF16)
+        bc = last_columns[:, :2 * STATE]
         bc_ref[...] = bc
+        raw = last_columns[:, 2 * STATE:].astype(F32) + db_ref[...]
         dt = jnp.maximum(raw, 0.0) + jnp.log1p(jnp.exp(-jnp.abs(raw)))
         logs = dt * an_ref[...]
         tri = (lax.broadcasted_iota(jnp.int32, (SEG, SEG), 0)
@@ -169,9 +167,9 @@
             log_copy(k).start()
         lall[me] = lsend[...]
 
-    @pl.when(at_lag(2))
-    def _():
-        core_copy(step - 2).start()
+    @pl.when(at_lag(3))
+    def _():
+        core_copy(step - 3).start()
 
     @pl.when(step == 2)
     def _():
@@ -191,15 +189,15 @@
         for c in range(tiles):
             drow[c] = spread(lane_shift(decays, c * TILE_HEADS + core * (TILE_HEADS // 2)), 2)
 
-    @pl.when(at_lag(3))
-    def _():
-        c = step - 3
+    @pl.when(at_lag(4))
+    def _():
+        c = step - 4
         core_copy(c).wait()
         sx[c] = drow[c, 0:1] * s_of(core == 0, c) + s_of(core == 1, c)
 
-    @pl.when(at_lag(4))
-    def _():
-        x_copy(step - 4).start()
+    @pl.when(at_lag(5))
+    def _():
+        x_copy(step - 5).start()
 
     @pl.when(at_lag(LAG_X))
     def _():
@@ -235,19 +233,17 @@
         hin_ref[:, :HALF] = jnp.where(core == 0, mine, got)
         hin_ref[:, HALF:] = jnp.where(core == 0, got, mine)
 
-    with_state = jnp.logical_and(step >= 1, step <= tiles)
+    with_state = jnp.logical_and(step >= 1, step <= tiles + 1)
 
     @pl.when(with_state)
     def _():
+        states(jnp.maximum(step - 2, 0))
         weigh(step - 1)
-        project_half(0)
-        states(step - 1)
-        project_half(1)
+        project()
 
     @pl.when(jnp.logical_not(with_state))
     def _():
-        for h in range(2):
-            project_half(h)
+        project()
 
     @pl.when(step == 2 * tiles - 1)
     def _():
@@ -397,20 +393,19 @@
             ],
             out_specs=[
                 pl.BlockSpec((tokens, TILE), lambda i: (0, lax.rem(i + tiles, 2 * tiles))),
-                pl.BlockSpec(((segs - 1) * STATE, TILE), lambda i: (0, jnp.clip(i - 1, 0, tiles - 1))),
+                pl.BlockSpec(((segs - 1) * STATE, TILE), lambda i: (0, jnp.clip(i - 2, 0, tiles - 1))),
                 pl.BlockSpec((STATE, TILE), lambda i: (0, jnp.maximum(i - (LAG_Y + 2), 0))),
                 any_space, any_space, any_space, any_space,
             ],
             scratch_shapes=[
                 pltpu.VMEM((tokens, d_model), BF16),
-                pltpu.VMEM((d_model, 2 * STATE), BF16),
-                pltpu.VMEM((d_model, heads), BF16),
+                pltpu.VMEM((d_model, 2 * STATE + heads), BF16),
                 pltpu.VMEM((1, heads), F32), pltpu.VMEM((1, heads), F32),
                 pltpu.VMEM((tokens, 2 * STATE), BF16),
                 pltpu.VMEM((tokens, heads), F32),
                 pltpu.VMEM((segs * heads, SEG), F32),
                 pltpu.VMEM((8, heads), F32),
-                pltpu.SemaphoreType.DMA((5,)), pltpu.SemaphoreType.DMA((4,)),
+                pltpu.SemaphoreType.DMA((4,)), pltpu.SemaphoreType.DMA((4,)),
                 pltpu.VMEM((segs * STATE, SEG), BF16),
                 pltpu.VMEM((8, heads), F32),
                 pltpu.VMEM((tokens, TILE), BF16),

time: 167 us -> 154 us (0.922)
  Pallas kernels: 167 us -> 154 us
    pallas_call x1, Pallas kernels: 113 us -> 100 us  [local_mixer(): pl.pallas_call(project_kernel, grid=(2 * tiles,), out_shape=[jax.ShapeDty...]
where the time goes in v3:
time: 154 us
  Pallas kernels  154 us (100%)
    pallas_call x1, Pallas kernels, local_mixer(): pl.pallas_call(project_kernel, grid=(2 * tiles,), out_shape=[jax.ShapeDty...  100 us
    pallas_call x1, Pallas kernels, local_mixer(): pl.pallas_call(mix_kernel, grid=(tiles // 2 + 1,), out_shape=jax.ShapeDty...  53.9 us

profile of v3, /device:TPU:0, one launch (start us, length us, event | category | flops | bytes accessed | tf_op | source)
XLA Modules:
  0.0 154.2 jit_solution(10432946998881162985)
XLA Ops:
  0.0 100.2 %project.1 = (bf16[512,16384]{1,0:T(8,128)(2,1)}, f32[384,8192]{1,0:T(8,128)}, f32[128,8192]{1,0:T(8,128)}, bf16[512,256]{1,0:T(8,128)(2,1)}, f32[512,128]{1,0:T...) custom-call(bf16[512,4096]{1,0:T(8,128)(2,1)} %x_hbm.3, bf16[4096,16768]{1,0:T(8,128)(2,1)} %w_hbm.2, ...), custom_call_target="tpu_custom_call" | custom-call | flops 70330089472 | bytes 137363456 | tf_op jit(solution)/shard_map/project/pallas_call | solution.py:377
  100.2 53.9 %mix.1 = bf16[512,4096]{1,0:T(8,128)(2,1)} custom-call(bf16[512,16384]{1,0:T(8,128)(2,1)} %get-tuple-element.12.z_ref.xs_ref, bf16[512,16384]{1,0:T(8,128)(2,1)} %get-tuple-element.12.z_ref.xs_ref, f32[384,8192]{1,0:T(8,128)} %get-tuple-element.13.loc_ref, f32[128,8192]{1,0:T(8,128)} %get-tuple-element.14.h_ref, bf16[512,256]{1,0:T(8,128)(2,1)} %get-tuple-element.15.bc_ref, ...), custom_call_target="tpu_custom_call" | custom-call | flops 34359738368 | bytes 67108864 | tf_op jit(solution)/shard_map/mix/pallas_call | solution.py:432

commit v4 on v3

--- a/solution.py
+++ b/solution.py
@@ -12,6 +12,7 @@
 HALF = TILE // 2
 TILE_HEADS = TILE // HEAD_DIM
 LANES = 128
+CHUNKS = 4
 LAG_X = 9
 LAG_Y = 14
 LOG2E = 1.4426950408889634
@@ -39,9 +40,9 @@
     return pltpu.roll(v, lax.rem(LANES - first, LANES), 1)
 
 
-def project_kernel(x_hbm, w_ref, w_hbm, an_hbm, db_hbm,
+def project_kernel(x_hbm, w_hbm, an_hbm, db_hbm,
                    u_ref, loc_ref, hin_ref, bc_hbm, gl_hbm, qt_hbm, dec_hbm,
-                   x_ref, wdt_ref, an_ref, db_ref, bc_ref, gl_ref, qt_ref, dec_ref, isem, osem,
+                   x_ref, wring, wdt_ref, an_ref, db_ref, bc_ref, gl_ref, qt_ref, dec_ref, isem, wsem, osem,
                    bt_ref, seg_dec, xw_ref, wst, uprev, drow, lsend, lall, s_own, rc, sx, rx, sy, ry, rf,
                    lsem, lrem, csem, crem, xsem, xrem, ysem, yrem, fsem, frem):
     step = pl.program_id(0)
@@ -50,12 +51,23 @@
     segs = tokens // SEG
     tiles = s_own.shape[0]
     heads_at = 2 * tiles * TILE
-    loads = [
+    depth = x_ref.shape[1] // CHUNKS
+    slots = wring.shape[0]
+    small_loads = [
         pltpu.make_async_copy(db_hbm, db_ref, isem.at[0]),
         pltpu.make_async_copy(an_hbm, an_ref, isem.at[1]),
-        pltpu.make_async_copy(x_hbm, x_ref, isem.at[2]),
-        pltpu.make_async_copy(w_hbm.at[:, heads_at:], wdt_ref, isem.at[3]),
     ]
+
+    def chunk_loads(q):
+        part = slice(q * depth, (q + 1) * depth)
+        return (pltpu.make_async_copy(x_hbm.at[:, part], x_ref.at[:, part], isem.at[2 + 2 * q]),
+                pltpu.make_async_copy(w_hbm.at[part, heads_at:], wdt_ref.at[part, :], isem.at[3 + 2 * q]))
+
+    def w_copy(at_step):
+        slot = lax.rem(at_step, slots)
+        first = pl.multiple_of(lax.rem(at_step + tiles, 2 * tiles) * TILE, TILE)
+        return pltpu.make_async_copy(w_hbm.at[:, pl.ds(first, TILE)], wring.at[slot], wsem.at[slot])
+
     stores = [
         pltpu.make_async_copy(bc_ref, bc_hbm, osem.at[0]),
         pltpu.make_async_copy(gl_ref, gl_hbm, osem.at[1]),
@@ -115,20 +127,33 @@
         s_own[tile, 0] = state[:, :HALF]
         s_own[tile, 1] = state[:, HALF:]
 
-    def project():
-        u = dot32(x_ref[...], w_ref[...]).astype(BF16)
+    def project(keep):
+        u = dot32(x_ref[...], wring[lax.rem(step, slots)]).astype(BF16)
         u_ref[...] = u
-        uprev[...] = u
+        if keep:
+            uprev[...] = u
 
     @pl.when(step == 0)
     def _():
         for k in range(1, 8):
             pl.semaphore_signal(barrier, inc=1, device_id={"sp": other(k)}, device_id_type=MESH)
-        for load in loads:
+        for q in range(CHUNKS):
+            for load in chunk_loads(q):
+                load.start()
+        for load in small_loads:
             load.start()
-        for load in loads:
+        for k in range(slots):
+            w_copy(k).start()
+        for load in small_loads:
             load.wait()
-        last_columns = dot32(x_ref[...], wdt_ref[...]).astype(BF16)
+        last_columns = None
+        for q in range(CHUNKS):
+            for load in chunk_loads(q):
+                load.wait()
+            part = slice(q * depth, (q + 1) * depth)
+            term = dot32(x_ref[:, part], wdt_ref[part, :])
+            last_columns = term if last_columns is None else last_columns + term
+        last_columns = last_columns.astype(BF16)
         bc = last_columns[:, :2 * STATE]
         bc_ref[...] = bc
         raw = last_columns[:, 2 * STATE:].astype(F32) + db_ref[...]
@@ -158,7 +183,7 @@
     def s_of(mine, c):
         return jnp.where(mine, s_own[c, core], rc[c])
 
-    @pl.when(step == 1)
+    @pl.when(step == 2)
     def _():
         pl.semaphore_wait(barrier, 7)
         for store in stores:
@@ -171,7 +196,7 @@
     def _():
         core_copy(step - 3).start()
 
-    @pl.when(step == 2)
+    @pl.when(step == 4)
     def _():
         for k in range(1, 8):
             log_copy(k).wait_send()
@@ -237,13 +262,24 @@
 
     @pl.when(with_state)
     def _():
+        w_copy(step).wait()
         states(jnp.maximum(step - 2, 0))
         weigh(step - 1)
-        project()
-
-    @pl.when(jnp.logical_not(with_state))
-    def _():
-        project()
+        project(True)
+
+    @pl.when(step == 0)
+    def _():
+        w_copy(step).wait()
+        project(True)
+
+    @pl.when(step > tiles + 1)
+    def _():
+        w_copy(step).wait()
+        project(False)
+
+    @pl.when(step + slots < 2 * tiles)
+    def _():
+        w_copy(step + slots).start()
 
     @pl.when(step == 2 * tiles - 1)
     def _():
@@ -387,9 +423,7 @@
                 jax.ShapeDtypeStruct((8, heads), F32),
             ],
             in_specs=[
-                any_space,
-                pl.BlockSpec((d_model, TILE), lambda i: (0, lax.rem(i + tiles, 2 * tiles))),
-                any_space, any_space, any_space,
+                any_space, any_space, any_space, any_space,
             ],
             out_specs=[
                 pl.BlockSpec((tokens, TILE), lambda i: (0, lax.rem(i + tiles, 2 * tiles))),
@@ -399,13 +433,14 @@
             ],
             scratch_shapes=[
                 pltpu.VMEM((tokens, d_model), BF16),
+                pltpu.VMEM((3, d_model, TILE), BF16),
                 pltpu.VMEM((d_model, 2 * STATE + heads), BF16),
                 pltpu.VMEM((1, heads), F32), pltpu.VMEM((1, heads), F32),
                 pltpu.VMEM((tokens, 2 * STATE), BF16),
                 pltpu.VMEM((tokens, heads), F32),
                 pltpu.VMEM((segs * heads, SEG), F32),
                 pltpu.VMEM((8, heads), F32),
-                pltpu.SemaphoreType.DMA((4,)), pltpu.SemaphoreType.DMA((4,)),
+                pltpu.SemaphoreType.DMA((2 + 2 * CHUNKS,)), pltpu.SemaphoreType.DMA((3,)), pltpu.SemaphoreType.DMA((4,)),
                 pltpu.VMEM((segs * STATE, SEG), BF16),
                 pltpu.VMEM((8, heads), F32),
                 pltpu.VMEM((tokens, TILE), BF16),
@@ -426,7 +461,7 @@
             cost_estimate=pl.CostEstimate(flops=2 * tokens * d_model * w_in.shape[1],
                                           bytes_accessed=2 * w_in.size, transcendentals=0),
             name="project",
-        )(x_loc, w_in, w_in, a_neg.reshape(1, heads), dt_bias.reshape(1, heads))
+        )(x_loc, w_in, a_neg.reshape(1, heads), dt_bias.reshape(1, heads))
 
         last = tiles // 2 - 1
         return pl.pallas_call(

time: 154 us -> 152 us (0.987)
  Pallas kernels: 154 us -> 151 us
    pallas_call x1, Pallas kernels: 100 us -> 97.5 us  [local_mixer(): pl.pallas_call(project_kernel, grid=(2 * tiles,), out_shape=[jax.ShapeDty...]
where the time goes in v4:
time: 152 us; the launch traced here: 151 us
  Pallas kernels  151 us (99%)
    pallas_call x1, Pallas kernels, local_mixer(): pl.pallas_call(project_kernel, grid=(2 * tiles,), out_shape=[jax.ShapeDty...  97.5 us
    pallas_call x1, Pallas kernels, local_mixer(): pl.pallas_call(mix_kernel, grid=(tiles // 2 + 1,), out_shape=jax.ShapeDty...  53.8 us

profile of v4, /device:TPU:0, one launch (start us, length us, event | category | flops | bytes accessed | tf_op | source)
XLA Modules:
  0.0 151.5 jit_solution(16493207733444194449)
XLA Ops:
  0.0 97.5 %project.1 = (bf16[512,16384]{1,0:T(8,128)(2,1)}, f32[384,8192]{1,0:T(8,128)}, f32[128,8192]{1,0:T(8,128)}, bf16[512,256]{1,0:T(8,128)(2,1)}, f32[512,128]{1,0:T...) custom-call(bf16[512,4096]{1,0:T(8,128)(2,1)} %x_hbm.3, bf16[4096,16768]{1,0:T(8,128)(2,1)} %w_hbm.2, f32[1,128]{1,0:T(1,128)} %bitcast.3, ...), custom_call_target="tpu_custom_call" | custom-call | flops 70330089472 | bytes 137363456 | tf_op jit(solution)/shard_map/project/pallas_call | solution.py:413
  97.5 53.8 %mix.1 = bf16[512,4096]{1,0:T(8,128)(2,1)} custom-call(bf16[512,16384]{1,0:T(8,128)(2,1)} %get-tuple-element.12.z_ref.xs_ref, bf16[512,16384]{1,0:T(8,128)(2,1)} %get-tuple-element.12.z_ref.xs_ref, f32[384,8192]{1,0:T(8,128)} %get-tuple-element.13.loc_ref, f32[128,8192]{1,0:T(8,128)} %get-tuple-element.14.h_ref, bf16[512,256]{1,0:T(8,128)(2,1)} %get-tuple-element.15.bc_ref, ...), custom_call_target="tpu_custom_call" | custom-call | flops 34359738368 | bytes 67108864 | tf_op jit(solution)/shard_map/mix/pallas_call | solution.py:467
